TPU v7x, 256 devices: a whole 4x4x8 slice. The times are simulated.
256 devices in a mesh: row: 8 (over y_lo, x), col: 32 (over z, y_hi, core).
Axes of the slice: x: 4, y: 4 (y_hi: 2, y_lo: 2; y = y_hi * 2 + y_lo), z: 8, core: 2. Of those that a mesh axis runs over, the one named last changes fastest.
Arguments:
- charge: float32 [256, 256, 256], P('col', 'row'), may hold values from -6 to 6
- green_spectrum: float32 [512, 512, 512], P('row', 'col'), may hold values from 0.2 to 2
Outputs:
- potential: float32 [256, 256, 256], P('col', 'row')
All inputs are finite; a program needn't handle non-finite values.
Results may differ from a plain program's by a relative error of at most 0.00007.
Values sent between devices are 32-bit elements; how exact they have to be, the bound alone decides.
A program may use at most 128 MiB of HBM per device.

v0:
```python
import math

import jax
import jax.numpy as jnp
from jax import lax
from jax.sharding import PartitionSpec as P

M = 512
N = 256


def in_blocks(value, dim, devices):
    lengths = value.shape
    parts = value.reshape(*lengths[:dim], devices, lengths[dim] // devices, *lengths[dim + 1 :])
    return jnp.moveaxis(parts, dim, 0)


def piece_ends(length, count):
    unit = 8 if length >= 8 * count else 1
    return [length // unit * k // count * unit for k in range(1, count)]


def in_order(parts, dim):
    parts = jnp.moveaxis(parts, 0, dim)
    lengths = parts.shape
    return parts.reshape(*lengths[:dim], lengths[dim] * lengths[dim + 1], *lengths[dim + 2 :])


def exchange_in_pieces(value, axis, pieces, split_dim, concat_dim):
    parts = in_blocks(value, split_dim, lax.axis_size(axis))
    cut = max(range(1, max(2, parts.ndim - 1)), key=lambda d: parts.shape[d])
    done = []
    for piece in jnp.split(parts, piece_ends(parts.shape[cut], pieces), axis=cut):
        if piece.size:
            done.append(lax.all_to_all(piece, axis, split_axis=0, concat_axis=0, tiled=True))
    return in_order(jnp.concatenate(done, axis=cut), concat_dim)


def phases(count_in, count_out, length):
    row_ids = lax.iota(jnp.int32, count_in)[:, None]
    col_ids = lax.iota(jnp.int32, count_out)[None, :]
    turn_ids = row_ids * col_ids % length
    angles = turn_ids.astype(jnp.float32) * (2.0 * math.pi / length)
    return (jnp.cos(angles), jnp.sin(angles))


def forward_table(count_in, count_out, length):
    cosine, sine_part = phases(count_in, count_out, length)
    return jnp.stack([jnp.stack([cosine, -sine_part], 1), jnp.stack([sine_part, cosine], 1)], 0)


def inverse_table(count_in, count_out, length):
    cosine, sine_part = phases(count_in, count_out, length)
    scaling = 1.0 / length
    return (
        jnp.stack([jnp.stack([cosine, sine_part], 1), jnp.stack([-sine_part, cosine], 1)], 0)
        * scaling
    )


def contract(pattern, left_side, right_side):
    return jnp.einsum(
        pattern,
        left_side,
        right_side,
        precision=lax.Precision.HIGHEST,
        preferred_element_type=jnp.float32,
    )


def on_device(charge, green_spectrum):
    cosine, sine_part = phases(N, M, M)
    real_table = jnp.stack([cosine, -sine_part], 1)
    along_z = contract("xyz,zqk->xyqk", charge, real_table)
    by_rows = exchange_in_pieces(along_z, "row", 2, 3, 1)
    forward = forward_table(N, M, M)
    along_y = contract("xypk,pyqb->xkqb", by_rows, forward)
    spectrum = contract(
        "xkpj,pxqa->kjqa",
        lax.all_to_all(along_y, "col", split_axis=3, concat_axis=0, tiled=True),
        forward,
    )
    product = spectrum * green_spectrum[:, :, None, :]
    back_table = inverse_table(M, N, M)
    back_cos, back_sin = phases(M, N, M)
    real_back = jnp.stack([back_cos, -back_sin], 0) * (1.0 / M)
    back_x = contract("kjqa,qapx->kjpx", product, back_table)
    by_cols = lax.all_to_all(back_x, "col", split_axis=3, concat_axis=1, tiled=True)
    back_y = contract("kbpx,pbqy->kxqy", by_cols, back_table)
    return contract(
        "cxpy,pcz->xyz",
        lax.all_to_all(back_y, "row", split_axis=3, concat_axis=0, tiled=True),
        real_back,
    )


def solution(mesh):
    in_specs = (P("col", "row", None), P("row", "col", None))
    out_specs = P("col", "row", None)
    return jax.shard_map(
        on_device, mesh=mesh, in_specs=in_specs, out_specs=out_specs, check_vma=False
    )
```

profile of v0, /device:TPU:1, one launch (start us, length us, event | category | flops | bytes accessed | tf_op | source)
XLA Modules:
  0.0 302.0 jit_solution(13520128151849072066)
XLA Ops:
  0.0 0.0 copy-start
  0.0 2.1 fusion.54
  2.1 0.0 copy-start.3
  2.1 0.0 copy-start.5
  2.1 0.8 copy-done.3
  2.9 0.2 copy-done.5
  3.1 0.0 copy-done
  3.1 1.1 convolution_bitcast_fusion
  4.2 0.4 reshape.228
  4.6 0.4 copy.82
  5.0 0.3 fusion.64
  5.3 1.4 reshape.245
  6.7 6.0 %all-to-all-start.1 = ((f32[8,1,16384]{2,1,0:T(1,128)}), f32[8,1,16384]{2,1,0:T(1,128)S(1)}, u32[]{:S(2)}, u32[]{:S(2)}) async-start(f32[8,1,16384]{2,1,0:T(1,128)} %reshape.245), calls=%async_computation.1 | async-start | bytes 1048576 | tf_op jit(solution)/shard_map/all_to_all | solution.py:35
  12.7 1.4 reshape.247
  14.2 8.8 %all-to-all-done.1 = f32[8,1,16384]{2,1,0:T(1,128)S(1)} async-done(((f32[8,1,16384]{2,1,0:T(1,128)}), f32[8,1,16384]{2,1,0:T(1,128)S(1)}, u32[]{:S(2)}, u32[]{:S(2)}) %all-to-all-start.1) | async-done | bytes 524320 | tf_op jit(solution)/shard_map/all_to_all | solution.py:35
  23.0 4.3 %all-to-all-start = ((f32[8,1,16384]{2,1,0:T(1,128)}), f32[8,1,16384]{2,1,0:T(1,128)}, u32[]{:S(2)}, u32[]{:S(2)}) async-start(f32[8,1,16384]{2,1,0:T(1,128)} %reshape.247), calls=%async_computation | async-start | bytes 1048576 | tf_op jit(solution)/shard_map/all_to_all | solution.py:35
  27.3 0.0 copy-done.8
  27.3 1.9 fusion.53
  29.2 0.0 copy-done.4
  29.2 0.0 copy-done.6
  29.2 0.3 fusion.29
  29.5 0.5 broadcast.343
  30.1 3.8 %reduce = f32[8,16384]{1,0:T(8,128)} reduce(f32[8,1,16384]{2,1,0:T(1,128)} %copy-done.8, f32[]{:T(128)} %broadcast.343), dimensions={1}, to_apply=%all_to_all.46.reduce_sub_computation | reduce | bytes 1048580 | tf_op jit(solution)/shard_map/all_to_all | solution.py:35
  33.9 1.5 reshape.246
  35.3 2.3 all-to-all-done
  37.6 3.8 %reduce.1 = f32[8,16384]{1,0:T(8,128)} reduce(f32[8,1,16384]{2,1,0:T(1,128)} %all-to-all-done, f32[]{:T(128)} %broadcast.343), dimensions={1}, to_apply=%all_to_all.45.reduce_sub_computation | reduce | bytes 1048580 | tf_op jit(solution)/shard_map/all_to_all | solution.py:35
  41.4 2.4 reshape.248
  43.8 1.5 maximum_bitcast_fusion
  45.3 0.2 copy.37
  45.6 5.2 %fusion.10 = f32[8,64,2,512]{3,1,2,0:T(8,128)} fusion(f32[8,256,2,64,1]{3,1,2,4,0:T(8,128)S(1)} %bitcast.118, f32[1,256,2,512]{3,1,2,0:T(8,128)S(1)} %get-tuple-element.10, f32[1,256,2,512]{3,1,2,0:T(8,128)S(1)} %get-tuple-element.9), kind=kOutput, calls=%fused_computation.15 | convolution fusion | flops 3221749760 | bytes 5242880 | tf_op jit(solution)/shard_map/xypk,pyqb->xkqb/dot_general | solution.py:62
  50.7 6.7 %copy.40 = f32[8,64,2,512]{1,2,0,3:T(2,128)} copy(f32[8,64,2,512]{3,1,2,0:T(8,128)} %fusion.10) | data formatting | bytes 4194304 | tf_op jit(solution)/shard_map/xypk,pyqb->xkqb/dot_general | solution.py:62
  57.4 6.6 %reshape.249 = f32[32,1,16384]{2,1,0:T(1,128)} reshape(f32[512,8,2,64]{3,2,1,0:T(2,128)} %bitcast.111) | data formatting | bytes 4194304
  64.0 11.8 %all-to-all-start.2 = ((f32[32,1,16384]{2,1,0:T(1,128)}), f32[32,1,16384]{2,1,0:T(1,128)}, u32[]{:S(2)}, u32[]{:S(2)}) async-start(f32[32,1,16384]{2,1,0:T(1,128)} %reshape.249), calls=%async_computation.2 | async-start | bytes 4194304 | tf_op jit(solution)/shard_map/all_to_all | solution.py:80
  75.7 1.9 fusion.56
  77.7 2.1 fusion.51
  79.7 0.2 maximum_bitcast_fusion.2
  79.9 45.9 %all-to-all-done.2 = f32[32,1,16384]{2,1,0:T(1,128)} async-done(((f32[32,1,16384]{2,1,0:T(1,128)}), f32[32,1,16384]{2,1,0:T(1,128)}, u32[]{:S(2)}, u32[]{:S(2)}) %all-to-all-start.2) | async-done | bytes 2097184 | tf_op jit(solution)/shard_map/all_to_all | solution.py:80
  125.8 8.7 %reduce.2 = f32[32,16384]{1,0:T(8,128)} reduce(f32[32,1,16384]{2,1,0:T(1,128)} %all-to-all-done.2, f32[]{:T(128)} %broadcast.343), dimensions={1}, to_apply=%all_to_all.47.reduce_sub_computation | reduce | bytes 4194308 | tf_op jit(solution)/shard_map/all_to_all | solution.py:80
  134.6 5.6 %reshape.250 = f32[512,8,2,64]{3,2,1,0:T(2,128)} reshape(f32[32,16384]{1,0:T(8,128)} %reduce.2) | data formatting | bytes 4194304
  140.2 3.5 %copy.41 = f32[8,64,2,512]{1,3,2,0:T(8,128)S(1)} copy(f32[8,64,2,512]{1,2,0,3:T(2,128)} %bitcast.113) | data formatting | bytes 4194304 | tf_op jit(solution)/shard_map/all_to_all | solution.py:80
  143.7 2.6 copy.42
  146.3 5.4 %copy.56 = f32[256,64,2,16,1]{0,3,2,4,1:T(8,128)} copy(f32[256,64,2,16,1]{1,3,2,0,4:T(8,128)} %bitcast.115) | data formatting | bytes 4194304 | tf_op jit(solution)/shard_map/all_to_all | solution.py:80
  151.7 0.0 copy-start.7
  151.7 9.3 %fusion.3 = f32[64,16,2,512,1]{3,1,4,2,0:T(8,128)S(1)} fusion(f32[256,64,2,16,1]{0,3,2,4,1:T(8,128)} %copy.56, f32[1,256,2,512]{3,1,2,0:T(8,128)} %copy-done.2, f32[1,256,2,512]{3,1,2,0:T(8,128)S(1)} %get-tuple-element.9), kind=kOutput, calls=%fused_computation.7 | convolution fusion | flops 6442975232 | bytes 8388608 | tf_op jit(solution)/shard_map/xkpj,pxqa->kjqa/dot_general | solution.py:62
  161.0 8.5 %fusion.13 = f32[64,16,2,256]{3,1,2,0:T(8,128)} fusion(f32[64,16,2,512,1]{3,1,4,2,0:T(8,128)S(1)} %fusion.3, f32[64,16,512]{2,1,0:T(8,128)S(1)} %copy-done.7, f32[1,512,2,256]{3,1,0,2:T(8,128)S(1)} %get-tuple-element.8, f32[1,512,2,256]{3,1,0,2:T(8,128)S(1)} %get-tuple-element.7), kind=kOutput, calls=%fused_computation.16 | convolution fusion | flops 6444548096 | bytes 10485760 | tf_op jit(solution)/shard_map/kjqa,qapx->kjpx/dot_general | solution.py:62
  169.6 5.6 %copy.46 = f32[64,16,2,256]{0,1,2,3:T(8,128)} copy(f32[64,16,2,256]{3,1,2,0:T(8,128)} %fusion.13) | data formatting | bytes 4194304 | tf_op jit(solution)/shard_map/kjqa,qapx->kjpx/dot_general | solution.py:62
  175.1 5.4 %reshape.251 = f32[32,1,16384]{2,1,0:T(1,128)} reshape(f32[256,2,16,64]{3,2,1,0:T(8,128)} %bitcast.112) | data formatting | bytes 4194304
  180.6 57.0 %all_to_all.64 = f32[32,1,16384]{2,1,0:T(1,128)} all-to-all(f32[32,1,16384]{2,1,0:T(1,128)} %reshape.251), channel_id=1, replica_groups=mesh['row'=8,'col'=32] {'col'}, dimensions={0} | all-to-all | bytes 4194304 | tf_op jit(solution)/shard_map/all_to_all | solution.py:88
  237.6 8.7 %reduce.3 = f32[32,16384]{1,0:T(8,128)} reduce(f32[32,1,16384]{2,1,0:T(1,128)} %all_to_all.64, f32[]{:T(128)} %broadcast.343), dimensions={1}, to_apply=%all_to_all.51.reduce_sub_computation | reduce | bytes 4194308 | tf_op jit(solution)/shard_map/all_to_all | solution.py:88
  246.3 4.2 %reshape.252 = f32[256,2,16,64]{3,2,1,0:T(8,128)} reshape(f32[32,16384]{1,0:T(8,128)} %reduce.3) | data formatting | bytes 4194304
  250.6 7.9 %copy.48 = f32[64,32,16,2,8]{0,4,3,2,1:T(8,128)} copy(f32[64,32,16,2,8]{0,2,3,4,1:T(8,128)} %bitcast.116) | data formatting | bytes 4194304 | tf_op jit(solution)/shard_map/all_to_all | solution.py:88
  258.5 4.7 %copy.60 = f32[64,512,2,8,1]{1,3,2,4,0:T(8,128)} copy(f32[64,512,2,8,1]{0,3,2,1,4:T(8,128)} %bitcast.117) | data formatting | bytes 4194304 | tf_op jit(solution)/shard_map/all_to_all | solution.py:88
  263.2 5.2 %fusion.19 = f32[64,8,2,256]{3,1,2,0:T(8,128)S(1)} fusion(f32[64,512,2,8,1]{1,3,2,4,0:T(8,128)} %copy.60, f32[1,512,2,256]{3,1,0,2:T(8,128)S(1)} %get-tuple-element.8, f32[1,512,2,256]{3,1,0,2:T(8,128)S(1)} %get-tuple-element.7), kind=kOutput, calls=%fused_computation.18 | convolution fusion | flops 3222274048 | bytes 5242880 | tf_op jit(solution)/shard_map/kbpx,pbqy->kxqy/dot_general | solution.py:62
  268.4 1.6 copy.50
  269.9 2.1 reshape.253
  272.1 3.6 %all-to-all-start.4 = ((f32[8,1,32768]{2,1,0:T(1,128)}), f32[8,1,32768]{2,1,0:T(1,128)S(1)}, u32[]{:S(2)}, u32[]{:S(2)}) async-start(f32[8,1,32768]{2,1,0:T(1,128)} %reshape.253), calls=%async_computation.4 | async-start | bytes 2097152 | tf_op jit(solution)/shard_map/all_to_all | solution.py:92
  275.6 2.9 sine_negate_fusion
  278.5 12.9 %all-to-all-done.4 = f32[8,1,32768]{2,1,0:T(1,128)S(1)} async-done(((f32[8,1,32768]{2,1,0:T(1,128)}), f32[8,1,32768]{2,1,0:T(1,128)S(1)}, u32[]{:S(2)}, u32[]{:S(2)}) %all-to-all-start.4) | async-done | bytes 1048608 | tf_op jit(solution)/shard_map/all_to_all | solution.py:92
  291.4 3.1 %reduce.4 = f32[8,32768]{1,0:T(8,128)S(1)} reduce(f32[8,1,32768]{2,1,0:T(1,128)S(1)} %all-to-all-done.4, f32[]{:T(128)} %broadcast.343), dimensions={1}, to_apply=%all_to_all.55.reduce_sub_computation | reduce | bytes 2097156 | tf_op jit(solution)/shard_map/all_to_all | solution.py:92
  294.6 0.8 reshape.254
  295.4 0.0 copy-start.1
  295.4 2.6 copy.52
  298.0 2.0 all_to_all.58
  300.0 1.7 convolution_bitcast_fusion.1
  (11 shorter events, 0.0 us)
Async XLA Ops:
  0.0 3.1 %copy-start = (f32[8,32,256]{2,1,0:T(8,128)S(1)}, f32[8,32,256]{2,1,0:T(8,128)}, u32[]{:S(2)}) copy-start(f32[8,32,256]{2,1,0:T(8,128)} %param.2) | copy-start | bytes 786436
  2.1 0.8 copy-start.3
  2.1 1.0 copy-start.5
  6.7 22.5 %copy-start.4 = (f32[256,1,512]{2,0,1:T(8,128)S(1)}, f32[256,1,512]{2,0,1:T(8,128)}, u32[]{:S(2)}) copy-start(f32[256,1,512]{2,0,1:T(8,128)} %copy-done.3) | copy-start | bytes 1572868
  6.7 22.5 %copy-start.6 = (f32[256,1,512]{2,0,1:T(8,128)S(1)}, f32[256,1,512]{2,0,1:T(8,128)}, u32[]{:S(2)}) copy-start(f32[256,1,512]{2,0,1:T(8,128)} %copy-done.5) | copy-start | bytes 1572868
  6.7 16.2 %all-to-all-start.1 = ((f32[8,1,16384]{2,1,0:T(1,128)}), f32[8,1,16384]{2,1,0:T(1,128)S(1)}, u32[]{:S(2)}, u32[]{:S(2)}) async-start(f32[8,1,16384]{2,1,0:T(1,128)} %reshape.245), calls=%async_computation.1 | async-start | bytes 1048576 | tf_op jit(solution)/shard_map/all_to_all | solution.py:35
  23.0 4.3 %copy-start.8 = (f32[8,1,16384]{2,1,0:T(1,128)}, f32[8,1,16384]{2,1,0:T(1,128)S(1)}, u32[]{:S(2)}) copy-start(f32[8,1,16384]{2,1,0:T(1,128)S(1)} %all-to-all-done.1) | copy-start | bytes 1572868
  23.0 14.7 %all-to-all-start = ((f32[8,1,16384]{2,1,0:T(1,128)}), f32[8,1,16384]{2,1,0:T(1,128)}, u32[]{:S(2)}, u32[]{:S(2)}) async-start(f32[8,1,16384]{2,1,0:T(1,128)} %reshape.247), calls=%async_computation | async-start | bytes 1048576 | tf_op jit(solution)/shard_map/all_to_all | solution.py:35
  29.5 16.0 %copy-start.2 = (f32[1,256,2,512]{3,1,2,0:T(8,128)}, f32[1,256,2,512]{3,1,2,0:T(8,128)S(1)}, u32[]{:S(2)}) copy-start(f32[1,256,2,512]{3,1,2,0:T(8,128)S(1)} %get-tuple-element.10) | copy-start | bytes 3145732
  64.0 61.9 %all-to-all-start.2 = ((f32[32,1,16384]{2,1,0:T(1,128)}), f32[32,1,16384]{2,1,0:T(1,128)}, u32[]{:S(2)}, u32[]{:S(2)}) async-start(f32[32,1,16384]{2,1,0:T(1,128)} %reshape.249), calls=%async_computation.2 | async-start | bytes 4194304 | tf_op jit(solution)/shard_map/all_to_all | solution.py:80
  151.7 9.3 %copy-start.7 = (f32[64,16,512]{2,1,0:T(8,128)S(1)}, f32[64,16,512]{2,1,0:T(8,128)}, u32[]{:S(2)}) copy-start(f32[64,16,512]{2,1,0:T(8,128)} %param.3) | copy-start | bytes 6291460
  272.1 19.4 %all-to-all-start.4 = ((f32[8,1,32768]{2,1,0:T(1,128)}), f32[8,1,32768]{2,1,0:T(1,128)S(1)}, u32[]{:S(2)}, u32[]{:S(2)}) async-start(f32[8,1,32768]{2,1,0:T(1,128)} %reshape.253), calls=%async_computation.4 | async-start | bytes 2097152 | tf_op jit(solution)/shard_map/all_to_all | solution.py:92
  295.4 6.3 %copy-start.1 = (f32[8,32,256]{2,1,0:T(8,128)S(1)}, f32[8,32,256]{2,1,0:T(8,128)}, u32[]{:S(2)}) copy-start(f32[8,32,256]{2,1,0:T(8,128)} %param.2) | copy-start | bytes 786436
  298.0 2.0 copy-start.9
  298.0 2.0 copy-start.10
where the time goes:
time: 308 us; the launch traced here: 302 us
  local copies, waits for them, and re-layouts  77 us (25%)
  waiting for transfers between devices  70 us (23%)
  blocking collectives  57 us (19%)
  other arithmetic  40.9 us (13%)
  matrix products  31 us (10%)
  starting transfers between devices  25.6 us (8%)
    all_to_all x1, blocking collectives, on_device(): lax.all_to_all(back_x, 'col', split_axis=3, concat_axis=1, tiled=True)  57 us
    all_to_all x1, waiting for transfers between devices, on_device(): lax.all_to_all(along_y, 'col', split_axis=3, concat_axis=0, tiled=True)  45.9 us
    unnamed x32, local copies, waits for them, and re-layouts  32.6 us
    dot_general x6, matrix products, contract(): jnp.einsum(pattern, left_side, right_side, precision=lax.Precision.HIGHES...  31 us
    dot_general x3, local copies, waits for them, and re-layouts, contract(): jnp.einsum(pattern, left_side, right_side, precision=lax.Precision.HIGHES...  13.8 us
    all_to_all x1, waiting for transfers between devices, on_device(): lax.all_to_all(back_y, 'row', split_axis=3, concat_axis=0, tiled=True)  12.9 us
    all_to_all x2, local copies, waits for them, and re-layouts, on_device(): lax.all_to_all(back_x, 'col', split_axis=3, concat_axis=1, tiled=True)  12.6 us
    all_to_all x1, starting transfers between devices, on_device(): lax.all_to_all(along_y, 'col', split_axis=3, concat_axis=0, tiled=True)  11.8 us
  transfers between devices with their start and end apart: 4, of which 4 were waited for; matrix products, arithmetic and copies ran while one was open for 5% of the time, Pallas kernels for 0%

commit v1 on v0

v1 whole, which is shorter than its diff:
```python
import functools
import math

import jax
import jax.numpy as jnp
import numpy as np
from jax import lax
from jax.experimental import pallas as pl
from jax.experimental.pallas import tpu as pltpu
from jax.sharding import PartitionSpec as P

M = 512
N = 256
ROWS = 8
COLS = 32
CHUNKS = 4
CW = M // ROWS // CHUNKS
MESH = pl.DeviceIdType.MESH


def halves(table):
    high = table.astype(jnp.bfloat16)
    low = (table - high.astype(np.float32)).astype(jnp.bfloat16)
    return np.stack([high, low])


def tables():
    turns = np.arange(N)[:, None] * np.arange(M)[None, :] % M
    angles = turns * (2.0 * np.pi / M)
    cosine, sine = np.cos(angles), np.sin(angles)
    parts = np.stack([cosine, -sine], 1).reshape(N, 2, ROWS, CHUNKS, CW)
    z_table = parts.transpose(3, 0, 1, 4, 2).reshape(CHUNKS, N, 2 * CW * ROWS)
    full = np.concatenate(
        [np.concatenate([cosine, -sine], 1), np.concatenate([sine, cosine], 1)], 0
    )
    return halves(z_table.astype(np.float32)), halves(full.astype(np.float32))


def split(value):
    high = value.astype(jnp.bfloat16)
    low = (value - high.astype(jnp.float32)).astype(jnp.bfloat16)
    return high, low


def product(left, right, dims):
    def one(a, b):
        return lax.dot_general(a, b, (dims, ((), ())), preferred_element_type=jnp.float32)

    return one(left[0], right[0]) + (one(left[0], right[1]) + one(left[1], right[0]))


def swap_groups(parts, width):
    parts = list(parts)
    count = len(parts)
    lanes = parts[0].shape[-1]
    step = 1
    while step < count:
        shift = step * width
        lane = lax.broadcasted_iota(jnp.int32, parts[0].shape, len(parts[0].shape) - 1)
        upper = (lane // shift) % 2 == 1
        axis = len(parts[0].shape) - 1
        for i in range(count):
            if i & step:
                continue
            one, two = parts[i], parts[i | step]
            parts[i] = jnp.where(upper, pltpu.roll(two, shift, axis), one)
            parts[i | step] = jnp.where(upper, two, pltpu.roll(one, lanes - shift, axis))
        step *= 2
    return parts


def body(
    charge, green, ztab_h, full_h, out, cells, gvm, ztab, full, row_out, row_in, col_out, col_in,
    back_out, back_in, last_out, last_in, load, s_row, r_row, s_col, r_col, s_back, r_back,
    s_last, r_last,
):
    row, col = lax.axis_index("row"), lax.axis_index("col")
    barrier = pltpu.get_barrier_semaphore()
    loads = [
        pltpu.make_async_copy(src, dst, load.at[k])
        for k, (src, dst) in enumerate(
            [(charge, cells), (ztab_h, ztab), (full_h, full), (green, gvm)]
        )
    ]
    for one in loads:
        one.start()

    def row_peer(k):
        return (row + k) % ROWS

    def col_peer(k):
        return (col + k) % COLS

    @pl.loop(1, ROWS)
    def _(k):
        pl.semaphore_signal(barrier, inc=1, device_id={"row": row_peer(k)}, device_id_type=MESH)

    @pl.loop(1, COLS)
    def _(k):
        pl.semaphore_signal(barrier, inc=1, device_id={"col": col_peer(k)}, device_id_type=MESH)

    def send(source, target, s_sem, r_sem, axis, j):
        count, me, peer = (ROWS, row, row_peer) if axis == "row" else (COLS, col, col_peer)

        @pl.loop(1, count)
        def _(k):
            to = peer(k)
            pltpu.make_async_remote_copy(
                src_ref=source.at[j, to],
                dst_ref=target.at[j, me],
                send_sem=s_sem.at[j],
                recv_sem=r_sem.at[j],
                device_id={axis: to},
                device_id_type=MESH,
            ).start()

    def await_all(ref, sem, j):
        view = ref.at[j, pl.ds(0, ref.shape[1] - 1)]
        pltpu.make_async_copy(view, view, sem.at[j]).wait()

    loads[0].wait()
    loads[1].wait()
    cells_h, cells_l = split(cells[...].reshape(8 * 32, N))
    pl.semaphore_wait(barrier, ROWS - 1 + COLS - 1)

    @pl.loop(0, CHUNKS)
    def _(j):
        along_z = product((cells_h, cells_l), (ztab[0, j], ztab[1, j]), ((1,), (0,)))
        for q in range(2):
            block = along_z[:, q * 128 : q * 128 + 128]
            pieces = swap_groups([block[x * 32 : x * 32 + 32] for x in range(8)], 1)
            for r in range(ROWS):
                row_out[j, r, q] = pieces[r]
        row_in[j, row] = row_out[j, row]
        send(row_out, row_in, s_row, r_row, "row", j)

    loads[2].wait()

    @pl.loop(0, CHUNKS)
    def _(j):
        await_all(row_in, r_row, j)
        data = jnp.concatenate([row_in[j, :, q].reshape(N, 128) for q in range(2)], 0)
        along_y = product(split(data.T), (full[0], full[1]), ((1,), (0,)))
        along_y = along_y.reshape(2, 8, 8, 2 * M)
        for v in range(8):
            q, high = v // 4, v % 4
            block = along_y[..., v * 128 : v * 128 + 128]
            pieces = swap_groups([block[:, i].reshape(16, 128) for i in range(8)], 16)
            for low in range(8):
                col_out[j, high * 8 + low, q] = pieces[low].reshape(2, 8, 128)
        col_in[j, col] = col_out[j, col]
        send(col_out, col_in, s_col, r_col, "col", j)

    loads[3].wait()

    @pl.loop(0, CHUNKS)
    def _(j):
        await_all(col_in, r_col, j)
        halves_x = []
        for h in range(2):
            data = jnp.concatenate([col_in[j, :, q, h].reshape(N, 128) for q in range(2)], 0)
            spectrum = product(split(data.T), (full[0], full[1]), ((1,), (0,)))
            weight = gvm[pl.ds(j * CW + h * 8, 8)].reshape(128, M)
            scaled = spectrum * jnp.concatenate([weight, weight], 1)
            halves_x.append(product(split(scaled), (full[0], full[1]), ((1,), (1,))))
        for v in range(4):
            q, high = v // 2, v % 2
            pieces = swap_groups(
                [
                    halves_x[i // 8][(i % 8) * 16 : (i % 8) * 16 + 16, v * 128 : v * 128 + 128]
                    for i in range(16)
                ],
                8,
            )
            for low in range(16):
                back_out[j, high * 16 + low, q] = pieces[low]
        back_in[j, col] = back_out[j, col]
        send(back_out, back_in, s_back, r_back, "col", j)

    @pl.loop(0, CHUNKS)
    def _(j):
        await_all(back_in, r_back, j)
        data = jnp.concatenate([back_in[j, :, q].reshape(M, 128) for q in range(2)], 0)
        back_y = product((full[0], full[1]), split(data), ((1,), (0,)))
        for q in range(2):
            for r in range(ROWS):
                last_out[j, r, q] = back_y[q * N + r * 32 : q * N + r * 32 + 32]
        last_in[j, row] = last_out[j, row]
        send(last_out, last_in, s_last, r_last, "row", j)

    out[...] = jnp.zeros_like(out)

    @pl.loop(0, CHUNKS)
    def _(j):
        await_all(last_in, r_last, j)
        parts = []
        for q in range(2):
            pieces = swap_groups([last_in[j, r, q] for r in range(ROWS)], 1)
            parts.append(jnp.concatenate(pieces, 0))
        data = jnp.concatenate(parts, 1)
        out[...] += product(split(data), (ztab[0, j], ztab[1, j]), ((1,), (1,)))

    @pl.loop(0, CHUNKS)
    def _(j):
        await_all(row_out, s_row, j)
        await_all(col_out, s_col, j)
        await_all(back_out, s_back, j)
        await_all(last_out, s_last, j)


def on_device(charge, green_spectrum):
    z_table, full_table = tables()
    any_space = pl.BlockSpec(memory_space=pl.ANY)
    field = pl.pallas_call(
        body,
        out_shape=jax.ShapeDtypeStruct((8 * 32, N), jnp.float32),
        in_specs=[any_space] * 4,
        out_specs=pl.BlockSpec(memory_space=pltpu.VMEM),
        scratch_shapes=[
            pltpu.VMEM((8, 32, N), jnp.float32),
            pltpu.VMEM((64, 16, M), jnp.float32),
            pltpu.VMEM(z_table.shape, jnp.bfloat16),
            pltpu.VMEM(full_table.shape, jnp.bfloat16),
            pltpu.VMEM((CHUNKS, ROWS, 2, 32, 128), jnp.float32),
            pltpu.VMEM((CHUNKS, ROWS, 2, 32, 128), jnp.float32),
            pltpu.VMEM((CHUNKS, COLS, 2, 2, 8, 128), jnp.float32),
            pltpu.VMEM((CHUNKS, COLS, 2, 2, 8, 128), jnp.float32),
            pltpu.VMEM((CHUNKS, COLS, 2, 16, 128), jnp.float32),
            pltpu.VMEM((CHUNKS, COLS, 2, 16, 128), jnp.float32),
            pltpu.VMEM((CHUNKS, ROWS, 2, 32, 128), jnp.float32),
            pltpu.VMEM((CHUNKS, ROWS, 2, 32, 128), jnp.float32),
            pltpu.SemaphoreType.DMA((4,)),
        ]
        + [pltpu.SemaphoreType.DMA((CHUNKS,))] * 8,
        compiler_params=pltpu.CompilerParams(
            collective_id=0, has_side_effects=True, vmem_limit_bytes=56 * 2**20
        ),
        name="poisson",
    )(charge, green_spectrum, z_table, full_table)
    return (field * (1.0 / M**3)).reshape(8, 32, N)


def solution(mesh):
    in_specs = (P("col", "row", None), P("row", "col", None))
    out_specs = P("col", "row", None)
    return jax.shard_map(
        on_device, mesh=mesh, in_specs=in_specs, out_specs=out_specs, check_vma=False
    )
```

time: 308 us -> 120 us (0.39); the launches traced: 302 us -> 120 us
  Pallas kernels: 0 us -> 119 us
  local copies, waits for them, and re-layouts: 77 us -> 0 us
  waiting for transfers between devices: 70 us -> 0 us
  blocking collectives: 57 us -> 0 us
  other arithmetic: 40.9 us -> 1.67 us
  matrix products: 31 us -> 0 us
  starting transfers between devices: 25.6 us -> 0 us
    pallas_call x0 -> x1, Pallas kernels: none -> 119 us  [on_device(): pl.pallas_call(body, out_shape=jax.ShapeDtypeStruct((8 * 32, N), jnp.floa...]
    all_to_all x4 -> x0, waiting for transfers between devices: 70 us -> none  [the longest x1 45.9 us: on_device(): lax.all_to_all(along_y, 'col', split_axis=3, concat_axis=0, tiled=True)]
    all_to_all x1 -> x0, blocking collectives: 57 us -> none  [on_device(): lax.all_to_all(back_x, 'col', split_axis=3, concat_axis=1, tiled=True)]
    unnamed x32 -> x0, local copies, waits for them, and re-layouts: 32.6 us -> none
    dot_general x6 -> x0, matrix products: 31 us -> none  [contract(): jnp.einsum(pattern, left_side, right_side, precision=lax.Precision.HIGHES...]
    all_to_all x8 -> x0, local copies, waits for them, and re-layouts: 29.2 us -> none  [the longest x2 12.6 us: on_device(): lax.all_to_all(back_x, 'col', split_axis=3, concat_axis=1, tiled=True)]
    all_to_all x5 -> x0, other arithmetic: 28.1 us -> none  [the longest x1 8.73 us: on_device(): lax.all_to_all(back_x, 'col', split_axis=3, concat_axis=1, tiled=True)]
    all_to_all x4 -> x0, starting transfers between devices: 25.6 us -> none  [the longest x1 11.8 us: on_device(): lax.all_to_all(along_y, 'col', split_axis=3, concat_axis=0, tiled=True)]
  transfers between devices with their start and end apart: 4 -> 0, of which waited for: 4 -> 0; matrix products, arithmetic and copies ran while one was open for 5% -> 0% of each run, Pallas kernels for 0% -> 0%
where the time goes in v1:
time: 120 us
  Pallas kernels  119 us (99%)
  other arithmetic  1.67 us (1%)
    pallas_call x1, Pallas kernels, on_device(): pl.pallas_call(body, out_shape=jax.ShapeDtypeStruct((8 * 32, N), jnp.floa...  119 us

profile of v1, /device:TPU:1, one launch (start us, length us, event | category | flops | bytes accessed | tf_op | source)
XLA Modules:
  0.0 120.3 jit_solution(5558443385796281933)
XLA Ops:
  0.0 118.6 %poisson.1 = f32[256,256]{1,0:T(8,128)} custom-call(f32[8,32,256]{2,1,0:T(8,128)} %charge.1, f32[64,16,512]{2,1,0:T(8,128)} %green.1, bf16[2,4,256,256]{3,2,1,0:T(8,128)(2,1)} %constant.6.clone.ztab_h, bf16[2,512,1024]{2,1,0:T(8,128)(2,1)} %constant.7.clone.full_h), custom_call_target="tpu_custom_call" | custom-call | tf_op jit(solution)/shard_map/poisson/pallas_call | solution.py:214
  118.6 1.7 %broadcast_multiply_fusion = f32[256,256]{1,0:T(8,128)} fusion(f32[256,256]{1,0:T(8,128)} %poisson.1), kind=kLoop, calls=%fused_computation | loop fusion | flops 65536 | bytes 524288 | tf_op jit(solution)/shard_map/mul | solution.py:240

commit v2 on v1

v2 whole, which is shorter than its diff:
```python
import functools
import math

import jax
import jax.numpy as jnp
import numpy as np
from jax import lax
from jax.experimental import pallas as pl
from jax.experimental.pallas import tpu as pltpu
from jax.sharding import PartitionSpec as P

M = 512
N = 256
ROWS = 8
COLS = 32
CHUNKS = 4
CW = M // ROWS // CHUNKS
MESH = pl.DeviceIdType.MESH


def halves(table):
    high = table.astype(jnp.bfloat16)
    low = (table - high.astype(np.float32)).astype(jnp.bfloat16)
    return np.stack([high, low])


def tables():
    turns = np.arange(N)[:, None] * np.arange(M)[None, :] % M
    angles = turns * (2.0 * np.pi / M)
    cosine, sine = np.cos(angles), np.sin(angles)
    parts = np.stack([cosine, -sine], 1).reshape(N, 2, ROWS, 2, CW, 2)
    z_table = parts.transpose(5, 3, 0, 1, 4, 2).reshape(CHUNKS, N, 2 * CW * ROWS)
    order = np.arange(N).reshape(ROWS, 2, CW).transpose(1, 2, 0).reshape(N)
    gap = 2 * (order[None, :] - order[:, None]) + 1
    bridge = 2.0 / N / (1.0 - np.exp(-2j * np.pi * gap / M))
    return (
        halves(z_table.astype(np.float32)),
        halves(np.stack([cosine, sine]).astype(np.float32)),
        halves(np.stack([bridge.real, bridge.imag]).astype(np.float32)),
    )


def split(value):
    high = value.astype(jnp.bfloat16)
    low = (value - high.astype(jnp.float32)).astype(jnp.bfloat16)
    return high, low


def product(left, right, dims):
    def one(a, b):
        return lax.dot_general(a, b, (dims, ((), ())), preferred_element_type=jnp.float32)

    return one(left[0], right[0]) + (one(left[0], right[1]) + one(left[1], right[0]))


def swap_groups(parts, width):
    parts = list(parts)
    count = len(parts)
    lanes = parts[0].shape[-1]
    step = 1
    while step < count:
        shift = step * width
        lane = lax.broadcasted_iota(jnp.int32, parts[0].shape, len(parts[0].shape) - 1)
        upper = (lane // shift) % 2 == 1
        axis = len(parts[0].shape) - 1
        for i in range(count):
            if i & step:
                continue
            one, two = parts[i], parts[i | step]
            parts[i] = jnp.where(upper, pltpu.roll(two, shift, axis), one)
            parts[i | step] = jnp.where(upper, two, pltpu.roll(one, lanes - shift, axis))
        step *= 2
    return parts


def body(
    charge, green, ztab_h, wave_h, bridge_h, out, cells, gvm, ztab, full, bridge,
    row_out, row_in, col_out, col_in, back_out, back_in, last_out, last_in,
    even_in, odd_out, odd_in, even_out, fold_in, load,
    s_row, r_row, s_col, r_col, s_back, r_back, s_last, r_last,
    s_even, r_even, s_odd, r_odd, s_fold, r_fold, s_ret, r_ret,
):
    row, col = lax.axis_index("row"), lax.axis_index("col")
    barrier = pltpu.get_barrier_semaphore()
    low, high = pl.ds(0, N), pl.ds(N, N)
    left, right = pl.ds(0, M), pl.ds(M, M)
    pairs = [
        (charge, cells),
        (ztab_h, ztab),
        (wave_h.at[:, 0], full.at[:, low, left]),
        (wave_h.at[:, 0], full.at[:, high, right]),
        (wave_h.at[:, 1], full.at[:, high, left]),
        (bridge_h.at[:, 0], bridge.at[:, low, low]),
        (bridge_h.at[:, 0], bridge.at[:, high, high]),
        (bridge_h.at[:, 1], bridge.at[:, low, high]),
        (green, gvm),
    ]
    loads = [
        pltpu.make_async_copy(src, dst, load.at[k]) for k, (src, dst) in enumerate(pairs)
    ]

    def row_peer(k):
        return (row + k) % ROWS

    def col_peer(k):
        return (col + k) % COLS

    @pl.loop(1, COLS)
    def _(k):
        pl.semaphore_signal(barrier, inc=1, device_id={"col": col_peer(k)}, device_id_type=MESH)

    @pl.loop(1, ROWS)
    def _(k):
        pl.semaphore_signal(barrier, inc=1, device_id={"row": row_peer(k)}, device_id_type=MESH)

    for one in loads:
        one.start()

    def send_row(source, target, s_sem, r_sem):
        @pl.loop(1, ROWS)
        def _(k):
            to = row_peer(k)
            pltpu.make_async_remote_copy(
                src_ref=source(to),
                dst_ref=target,
                send_sem=s_sem,
                recv_sem=r_sem,
                device_id={"row": to},
                device_id_type=MESH,
            ).start()

    def send_col(source, target, s_sem, r_sem, j, half):
        target[j, half, col] = source[j, half, col]

        @pl.loop(1, COLS)
        def _(k):
            to = col_peer(k)
            pltpu.make_async_remote_copy(
                src_ref=source.at[j, half, to],
                dst_ref=target.at[j, half, col],
                send_sem=s_sem.at[2 * j + half],
                recv_sem=r_sem.at[2 * j + half],
                device_id={"col": to},
                device_id_type=MESH,
            ).start()

    def await_bytes(view, sem):
        pltpu.make_async_copy(view, view, sem).wait()

    def await_row(ref, sem, j):
        await_bytes(ref.at[j, pl.ds(0, ROWS - 1)], sem.at[j])

    def await_col(ref, sem, j, half):
        await_bytes(ref.at[j, half, pl.ds(0, COLS - 1)], sem.at[2 * j + half])

    loads[0].wait()
    loads[1].wait()
    cells_h, cells_l = split(cells[...].reshape(8 * 32, N))

    @pl.loop(0, CHUNKS)
    def _(j):
        along_z = product((cells_h, cells_l), (ztab[0, j], ztab[1, j]), ((1,), (0,)))
        for q in range(2):
            block = along_z[:, q * 128 : q * 128 + 128]
            pieces = swap_groups([block[x * 32 : x * 32 + 32] for x in range(8)], 1)
            for r in range(ROWS):
                row_out[j, r, q] = pieces[r]

    pl.semaphore_wait(barrier, ROWS - 1 + COLS - 1)

    @pl.loop(0, CHUNKS)
    def _(j):
        send_row(lambda to: row_out.at[j, to], row_in.at[j, row], s_row.at[j], r_row.at[j])
        row_in[j, row] = row_out[j, row]

    for one in loads[2:8]:
        one.wait()
    full[:, 0:N, M:] = -full[:, N:, 0:M]
    bridge[:, N:, 0:N] = -bridge[:, 0:N, N:]

    @pl.loop(0, CHUNKS)
    def _(j):
        await_row(row_in, r_row, j)
        data = jnp.concatenate([row_in[j, :, q].reshape(N, 128) for q in range(2)], 0)
        along_y = product(split(data.T), (full[0], full[1]), ((1,), (0,)))
        for v in range(8):
            q, top = v // 4, v % 4
            pieces = swap_groups(
                [along_y[i * 8 : i * 8 + 8, v * 128 : v * 128 + 128] for i in range(16)], 8
            )
            for g in range(16):
                col_out[j, g % 2, top * 8 + g // 2, q] = pieces[g]

        @pl.when(j < 2)
        def _():
            send_col(col_out, col_in, s_col, r_col, j, 0)

        @pl.when(j == 1)
        def _():
            send_col(col_out, col_in, s_col, r_col, 0, 1)

        @pl.when(j >= 1)
        def _():
            send_col(col_out, col_in, s_col, r_col, j, 1)

    loads[8].wait()
    for e in range(2):
        back_in[2 + e, 0] = jnp.zeros_like(back_in[2 + e, 0])

    def four(index):
        return pl.ds(index * 4, 4)

    def across(source, target, dims):
        parts = []
        for q in range(2):
            for e in range(2):
                pieces = [source[e, r, :, q].reshape(32, 128) for r in range(ROWS)]
                parts.append(jnp.concatenate(swap_groups(pieces, 1), 0))
        data = jnp.concatenate(parts, 1)
        moved = product(split(data), (bridge[0], bridge[1]), dims)
        for v in range(4):
            q, e = v // 2, v % 2
            block = moved[:, v * 128 : v * 128 + 128]
            pieces = swap_groups([block[k * 32 : k * 32 + 32] for k in range(8)], 1)
            for r in range(ROWS):
                target[e, r, :, q] = pieces[r].reshape(4, 8, 128)

    @pl.loop(0, 2 * CHUNKS)
    def _(s):
        j = s // 4 * 2 + s % 2
        half = s % 4 // 2
        e = s % 2

        @pl.when(s == 3)
        def _():
            for k in range(2):
                await_row(even_in, r_even, k)
            across(even_in, odd_out, ((1,), (0,)))
            for k in range(2):
                send_row(
                    lambda to: odd_out.at[k, to],
                    col_in.at[2 + k, 0, four(row)],
                    s_odd.at[k],
                    r_odd.at[k],
                )
                col_in[2 + k, 0, four(row)] = odd_out[k, row]

        @pl.when((j < 2) | (half == 1))
        def _():
            await_col(col_in, r_col, j, half)

        @pl.when((j >= 2) & (half == 0))
        def _():
            await_row(odd_in, r_odd, e)

        @pl.when(s < 2)
        def _():
            send_row(
                lambda to: col_in.at[e, 0, four(to)],
                even_in.at[e, row],
                s_even.at[e],
                r_even.at[e],
            )
            even_in[e, row] = col_in[e, 0, four(row)]

        data = jnp.concatenate([col_in[j, half, :, q].reshape(N, 128) for q in range(2)], 0)
        spectrum = product(split(data.T), (full[0], full[1]), ((1,), (0,)))
        weight = gvm[pl.ds(e * CW, CW), j // 2, half].reshape(128, M)
        scaled = spectrum * jnp.concatenate([weight, weight], 1)
        along_x = product(split(scaled), (full[0], full[1]), ((1,), (1,)))
        for v in range(4):
            q, top = v // 2, v % 2
            pieces = swap_groups(
                [along_x[i * 8 : i * 8 + 8, v * 128 : v * 128 + 128] for i in range(16)], 8
            )
            for g in range(16):
                back_out[j, half, top * 16 + g, q] = pieces[g]

        @pl.when(half == 1)
        def _():
            send_col(back_out, back_in, s_back, r_back, j, half)

        @pl.when((j >= 2) & (half == 0))
        def _():
            send_row(
                lambda to: back_out.at[j, 0, four(to)],
                odd_in.at[e, row],
                s_fold.at[e],
                r_fold.at[e],
            )
            odd_in[e, row] = back_out[j, 0, four(row)]

    for e in range(2):
        await_row(odd_in, r_fold, e)
    across(odd_in, even_out, ((1,), (1,)))
    for e in range(2):
        send_row(
            lambda to: even_out.at[e, to], fold_in.at[e, row], s_ret.at[e], r_ret.at[e]
        )
        fold_in[e, row] = even_out[e, row]
    for e in range(2):
        await_row(fold_in, r_ret, e)
        back_out[e, 0] = back_out[e, 0] + fold_in[e].reshape(COLS, 2, 8, 128)
        send_col(back_out, back_in, s_back, r_back, e, 0)

    @pl.loop(0, CHUNKS)
    def _(s):
        j = (s + 2) % CHUNKS
        await_col(back_in, r_back, j, 1)

        @pl.when(j < 2)
        def _():
            await_col(back_in, r_back, j, 0)

        data = jnp.concatenate(
            [
                jnp.stack([back_in[j, 0, :, q], back_in[j, 1, :, q]], 1).reshape(M, 128)
                for q in range(2)
            ],
            0,
        )
        back_y = product((full[0], full[1]), split(data), ((1,), (0,)))
        for q in range(2):
            for r in range(ROWS):
                last_out[j, r, q] = back_y[q * N + r * 32 : q * N + r * 32 + 32]
        send_row(lambda to: last_out.at[j, to], last_in.at[j, row], s_last.at[j], r_last.at[j])
        last_in[j, row] = last_out[j, row]

    out[...] = jnp.zeros_like(out)

    @pl.loop(0, CHUNKS)
    def _(s):
        j = (s + 2) % CHUNKS
        await_row(last_in, r_last, j)
        parts = []
        for q in range(2):
            pieces = swap_groups([last_in[j, r, q] for r in range(ROWS)], 1)
            parts.append(jnp.concatenate(pieces, 0))
        data = jnp.concatenate(parts, 1)
        out[...] += product(split(data), (ztab[0, j], ztab[1, j]), ((1,), (1,)))

    @pl.loop(0, CHUNKS)
    def _(j):
        await_row(row_out, s_row, j)
        await_row(last_out, s_last, j)
        await_col(col_out, s_col, j, 1)
        await_col(back_out, s_back, j, 1)

    @pl.loop(0, 2)
    def _(e):
        await_col(col_out, s_col, e, 0)
        await_col(back_out, s_back, e, 0)
        await_row(even_in, s_even, e)
        await_row(odd_out, s_odd, e)
        await_row(odd_in, s_fold, e)
        await_row(even_out, s_ret, e)


def on_device(charge, green_spectrum):
    z_table, wave, bridge = tables()
    any_space = pl.BlockSpec(memory_space=pl.ANY)
    row_buffer = pltpu.VMEM((CHUNKS, ROWS, 2, 32, 128), jnp.float32)
    col_buffer = pltpu.VMEM((CHUNKS, 2, COLS, 2, 8, 128), jnp.float32)
    side_buffer = pltpu.VMEM((2, ROWS, 4, 2, 8, 128), jnp.float32)
    field = pl.pallas_call(
        body,
        out_shape=jax.ShapeDtypeStruct((8 * 32, N), jnp.float32),
        in_specs=[any_space] * 5,
        out_specs=pl.BlockSpec(memory_space=pltpu.VMEM),
        scratch_shapes=[
            pltpu.VMEM((8, 32, N), jnp.float32),
            pltpu.VMEM((32, 2, 2, 8, M), jnp.float32),
            pltpu.VMEM(z_table.shape, jnp.bfloat16),
            pltpu.VMEM((2, 2 * N, 2 * M), jnp.bfloat16),
            pltpu.VMEM((2, 2 * N, 2 * N), jnp.bfloat16),
            row_buffer, row_buffer, col_buffer, col_buffer, col_buffer, col_buffer,
            row_buffer, row_buffer,
            side_buffer, side_buffer, side_buffer, side_buffer, side_buffer,
            pltpu.SemaphoreType.DMA((9,)),
            pltpu.SemaphoreType.DMA((CHUNKS,)),
            pltpu.SemaphoreType.DMA((CHUNKS,)),
        ]
        + [pltpu.SemaphoreType.DMA((2 * CHUNKS,))] * 4
        + [pltpu.SemaphoreType.DMA((CHUNKS,))] * 2
        + [pltpu.SemaphoreType.DMA((2,))] * 8,
        compiler_params=pltpu.CompilerParams(
            collective_id=0, has_side_effects=True, vmem_limit_bytes=56 * 2**20
        ),
        name="poisson",
    )(charge, green_spectrum.reshape(32, 2, 2, 8, M), z_table, wave, bridge)
    return (field * (1.0 / M**3)).reshape(8, 32, N)


def solution(mesh):
    in_specs = (P("col", "row", None), P("row", "col", None))
    out_specs = P("col", "row", None)
    return jax.shard_map(
        on_device, mesh=mesh, in_specs=in_specs, out_specs=out_specs, check_vma=False
    )
```

time: 120 us -> 104 us (0.87)
  Pallas kernels: 119 us -> 102 us
    pallas_call x1, Pallas kernels: 119 us -> 102 us  [on_device(): pl.pallas_call(body, out_shape=jax.ShapeDtypeStruct((8 * 32, N), jnp.floa...]
where the time goes in v2:
time: 104 us
  Pallas kernels  102 us (98%)
  other arithmetic  1.67 us (2%)
    pallas_call x1, Pallas kernels, on_device(): pl.pallas_call(body, out_shape=jax.ShapeDtypeStruct((8 * 32, N), jnp.floa...  102 us

profile of v2, /device:TPU:1, one launch (start us, length us, event | category | flops | bytes accessed | tf_op | source)
XLA Modules:
  0.0 104.1 jit_solution(966697347252582394)
XLA Ops:
  0.0 102.5 %poisson.1 = f32[256,256]{1,0:T(8,128)} custom-call(f32[8,32,256]{2,1,0:T(8,128)} %charge.1, f32[32,2,2,8,512]{4,3,2,1,0:T(8,128)} %bitcast.2, bf16[2,4,256,256]{3,2,1,0:T(8,128)(2,1)} %constant.8.clone.ztab_h, bf16[2,2,256,512]{3,2,1,0:T(8,128)(2,1)} %constant.9.clone.wave_h, bf16[2,2,256,256]{3,2,1,0:T(8,128)(2,1)} %constant.10.clone.bridge_h), custom_call_target="tpu_custom_call" | custom-call | tf_op jit(solution)/shard_map/poisson/pallas_call | solution.py:365
  102.5 1.7 %broadcast_multiply_fusion = f32[256,256]{1,0:T(8,128)} fusion(f32[256,256]{1,0:T(8,128)} %poisson.1), kind=kLoop, calls=%fused_computation | loop fusion | flops 65536 | bytes 524288 | tf_op jit(solution)/shard_map/mul | solution.py:391

commit v3 on v2

--- a/solution.py
+++ b/solution.py
@@ -231,7 +231,7 @@
         half = s % 4 // 2
         e = s % 2
 
-        @pl.when(s == 3)
+        @pl.when(s == 2)
         def _():
             for k in range(2):
                 await_row(even_in, r_even, k)
@@ -384,7 +384,7 @@
         + [pltpu.SemaphoreType.DMA((CHUNKS,))] * 2
         + [pltpu.SemaphoreType.DMA((2,))] * 8,
         compiler_params=pltpu.CompilerParams(
-            collective_id=0, has_side_effects=True, vmem_limit_bytes=56 * 2**20
+            collective_id=0, has_side_effects=True, vmem_limit_bytes=54800 * 2**10
         ),
         name="poisson",
     )(charge, green_spectrum.reshape(32, 2, 2, 8, M), z_table, wave, bridge)

time: 104 us -> 101 us (0.971)
  Pallas kernels: 102 us -> 99.9 us
    pallas_call x1, Pallas kernels: 102 us -> 99.9 us  [on_device(): pl.pallas_call(body, out_shape=jax.ShapeDtypeStruct((8 * 32, N), jnp.floa...]
where the time goes in v3:
time: 101 us
  Pallas kernels  99.9 us (99%)
    pallas_call x1, Pallas kernels, on_device(): pl.pallas_call(body, out_shape=jax.ShapeDtypeStruct((8 * 32, N), jnp.floa...  99.9 us

profile of v3, /device:TPU:1, one launch (start us, length us, event | category | flops | bytes accessed | tf_op | source)
XLA Modules:
  0.0 100.6 jit_solution(480696654599838179)
XLA Ops:
  0.0 99.9 %poisson.1 = f32[256,256]{1,0:T(8,128)S(1)} custom-call(f32[8,32,256]{2,1,0:T(8,128)} %charge.1, f32[32,2,2,8,512]{4,3,2,1,0:T(8,128)} %bitcast.2, bf16[2,4,256,256]{3,2,1,0:T(8,128)(2,1)} %constant.8.clone.ztab_h, bf16[2,2,256,512]{3,2,1,0:T(8,128)(2,1)} %constant.9.clone.wave_h, bf16[2,2,256,256]{3,2,1,0:T(8,128)(2,1)} %constant.10.clone.bridge_h), custom_call_target="tpu_custom_call" | custom-call | tf_op jit(solution)/shard_map/poisson/pallas_call | solution.py:365
  99.9 0.7 broadcast_multiply_fusion

commit v4 on v3

--- a/solution.py
+++ b/solution.py
@@ -103,7 +103,8 @@
         return (row + k) % ROWS
 
     def col_peer(k):
-        return (col + k) % COLS
+        ahead, behind = (k + 1) // 2, COLS - k // 2
+        return (col + k % 2 * ahead + (1 - k % 2) * behind) % COLS
 
     @pl.loop(1, COLS)
     def _(k):

time: 101 us -> 102 us (level)
  Pallas kernels: 99.9 us -> 102 us
    pallas_call x1, Pallas kernels: 99.9 us -> 102 us  [on_device(): pl.pallas_call(body, out_shape=jax.ShapeDtypeStruct((8 * 32, N), jnp.floa...]
where the time goes in v4:
time: 102 us
  Pallas kernels  102 us (100%)
    pallas_call x1, Pallas kernels, on_device(): pl.pallas_call(body, out_shape=jax.ShapeDtypeStruct((8 * 32, N), jnp.floa...  102 us

profile of v4, /device:TPU:1, one launch (start us, length us, event | category | flops | bytes accessed | tf_op | source)
XLA Modules:
  0.0 102.3 jit_solution(9352086526111928444)
XLA Ops:
  0.0 101.6 %poisson.1 = f32[256,256]{1,0:T(8,128)S(1)} custom-call(f32[8,32,256]{2,1,0:T(8,128)} %charge.1, f32[32,2,2,8,512]{4,3,2,1,0:T(8,128)} %bitcast.2, bf16[2,4,256,256]{3,2,1,0:T(8,128)(2,1)} %constant.8.clone.ztab_h, bf16[2,2,256,512]{3,2,1,0:T(8,128)(2,1)} %constant.9.clone.wave_h, bf16[2,2,256,256]{3,2,1,0:T(8,128)(2,1)} %constant.10.clone.bridge_h), custom_call_target="tpu_custom_call" | custom-call | tf_op jit(solution)/shard_map/poisson/pallas_call | solution.py:366
  101.6 0.7 broadcast_multiply_fusion
